TPU v7x, 32 devices: a whole 2x2x4 slice. The times are simulated.
32 devices in a mesh: cell: 16 (over z, y, x), pre: 2 (over core).
Axes of the slice: x: 2, y: 2, z: 4, core: 2. Of those that a mesh axis runs over, the one named last changes fastest.
Arguments:
- v_init: float32 [128, 16, 4096], P(None, None, ('cell', 'pre')), may hold values from -6 to 6
- cotangent: float32 [128, 16, 4096], P(None, None, ('cell', 'pre')), may hold values from -6 to 6
- weights: bfloat16 [4096, 4096], P('cell', 'pre'), may hold values from -2 to 2
- leak: float32 [4096], P(('cell', 'pre')), may hold values from 0.2 to 1.5
- drive: float32 [4096], P(('cell', 'pre')), may hold values from 0.5 to 2
- site: int32 [4096], P(('cell', 'pre')), may hold values from 0 to 127
- parent: int32 [128], replicated, may hold values from 0 to 126, as said below
- axial: float32 [128], replicated, may hold values from 1 to 8
- cap: float32 [128], replicated, may hold values from 2 to 6
- bank: float32 [16, 128], replicated, may hold values from -5 to 5
- sched: int32 [2, 16], replicated, may hold values from 0 to 15
Outputs:
- v_final: float32 [128, 16, 4096], P(None, None, ('cell', 'pre'))
- v_grad: float32 [128, 16, 4096], P(None, None, ('cell', 'pre'))
Inputs may be any that keep to these rules, and one draw needn't show every extreme that they name: parent[0] = 0, and for i >= 1 parent[i] < i and i - parent[i] <= 8.
All inputs are finite; a program needn't handle non-finite values.
Results may differ from a plain program's by a relative error of at most 0.0021.
Values may be sent and summed in bfloat16 or wider, within the bound.
A program may use at most 64 MiB of HBM per device.

v0:
```python
import jax
import jax.numpy as jnp
from jax import lax
from jax.sharding import PartitionSpec as P

reversal = 1.0


def tree_inverse(parent, axial, cap):
    length = parent.shape[0]
    indices = jnp.arange(length, dtype=jnp.int32)
    onehot = (parent[:, None] == indices[None, :]).astype(jnp.float32)
    ident = jnp.eye(length, dtype=jnp.float32)
    edges = (ident - onehot) * (indices > 0).astype(jnp.float32)[:, None]
    shunt = axial * (indices == 0).astype(jnp.float32)
    system = jnp.diag(cap + shunt) + jnp.dot(
        edges.T * axial[None, :], edges, precision=lax.Precision.HIGHEST
    )
    lower = jnp.linalg.cholesky(system)
    factor = lax.linalg.triangular_solve(lower, ident, left_side=True, lower=True)
    return jnp.dot(factor.T, factor, precision=lax.Precision.HIGHEST)


def apply_matrix(matrix, field):
    depth, trials, cells = field.shape
    flat = jnp.dot(matrix, field.reshape(depth, trials * cells), precision=lax.Precision.HIGHEST)
    return flat.reshape(depth, trials, cells)


def forward_drive(activity, weights):
    partial_rows = lax.dot_general(
        lax.all_gather(activity, "cell", axis=1, tiled=True),
        weights,
        (((1,), (1,)), ((), ())),
        preferred_element_type=jnp.float32,
    )
    return lax.psum_scatter(partial_rows, "pre", scatter_dimension=1, tiled=True)


def backward_drive(site_adjoint, weights):
    partial_cols = jnp.dot(
        lax.all_gather(site_adjoint, "pre", axis=1, tiled=True),
        weights,
        preferred_element_type=jnp.float32,
    )
    return lax.psum_scatter(partial_cols, "cell", scatter_dimension=1, tiled=True)


def body(v_init, cotangent, weights, leak, drive, site, parent, axial, cap, bank, sched):
    inverse = tree_inverse(parent, axial, cap)
    depth = parent.shape[0]
    comps = jnp.arange(depth, dtype=jnp.int32)
    mask = (site[None, :] == comps[:, None]).astype(jnp.float32)
    levels = cap[:, None, None] - leak[None, None, :]
    select = (
        sched[:, :, None] == jnp.arange(bank.shape[0], dtype=jnp.int32)[None, None, :]
    ).astype(jnp.float32)
    field = v_init
    saved = []
    for moment in range(sched.shape[0]):
        rates = jax.nn.sigmoid(field[0])
        activity = rates.astype(jnp.bfloat16)
        synaptic = forward_drive(activity, weights)
        pattern = jnp.dot(select[moment], bank, precision=lax.Precision.HIGHEST)
        source = pattern.T[:, :, None] * drive[None, None, :]
        total = levels * field + mask[:, None, :] * synaptic[None] * (reversal - field) + source
        saved.append((field, rates, synaptic))
        field = apply_matrix(inverse, total)
    adjoint = cotangent
    for moment in range(sched.shape[0] - 1, -1, -1):
        state, rates, synaptic = saved[moment]
        pulled = apply_matrix(inverse.T, adjoint)
        site_adjoint = jnp.sum(mask[:, None, :] * pulled * (reversal - state), axis=0).astype(
            jnp.bfloat16
        )
        returned = backward_drive(site_adjoint, weights)
        adjoint = levels * pulled - mask[:, None, :] * synaptic[None] * pulled
        adjoint = adjoint.at[0].add(returned * rates * (1.0 - rates))
    return (field, adjoint)


def solution(mesh):
    in_specs = (
        P(None, None, ("cell", "pre")),
        P(None, None, ("cell", "pre")),
        P("cell", "pre"),
        P(("cell", "pre")),
        P(("cell", "pre")),
        P(("cell", "pre")),
        P(),
        P(),
        P(),
        P(),
        P(),
    )
    out_specs = (P(None, None, ("cell", "pre")), P(None, None, ("cell", "pre")))
    return jax.shard_map(body, mesh=mesh, in_specs=in_specs, out_specs=out_specs, check_vma=False)
```

profile of v0, /device:TPU:0, one launch (start us, length us, event | category | flops | bytes accessed | tf_op | source)
XLA Modules:
  0.0 310.3 jit_solution(1017453609851802560)
XLA Ops:
  7.2 0.8 bitcast_convert_fusion
  8.0 42.7 %all_gather.12 = bf16[16,2048]{1,0:T(8,128)(2,1)S(1)} all-gather(bf16[16,128]{1,0:T(8,128)(2,1)S(1)} %bitcast_convert_fusion), channel_id=1, replica_groups=mesh['cell'=16,'pre'=2] {'cell'}, dimensions={1}, use_global_device_ids=true | all-gather | bytes 69632 | tf_op jit(solution)/shard_map/all_gather | solution.py:32
  50.8 1.0 fusion.42
  51.8 0.6 copy-done.7
  52.5 0.6 copy-done.8
  53.1 0.6 copy-done.9
  53.8 0.6 copy-done.10
  54.5 0.6 copy-done.11
  55.1 0.3 fusion.19
  55.6 11.7 %cholesky.18 = f32[128,128]{1,0:T(8,128)S(1)} custom-call(f32[128,128]{1,0:T(8,128)S(1)} %fusion.18), custom_call_target="Cholesky" | custom-call | tf_op jit(solution)/shard_map/jit(cholesky)/cholesky | solution.py:19
  67.3 0.6 compare_reduce_fusion
  68.0 0.7 fusion.8
  68.6 9.8 %custom-call.6 = f32[1,128,128]{1,2,0:T(8,128)S(1)} custom-call(f32[1,128,128]{2,1,0:T(8,128)S(1)} %fusion.8), custom_call_target="InvertDiagBlocksLowerTriangular" | custom-call | tf_op jit(solution)/shard_map/triangular_solve | solution.py:20
  78.5 0.2 fusion.15
  78.7 0.3 fusion.41
  79.0 0.4 copy-done.5
  79.4 0.1 convolution_bitcast_fusion
  79.5 0.1 convolution_bitcast_fusion.1
  79.7 0.5 copy-done.6
  80.2 1.1 fusion.1
  81.3 1.3 copy.35
  82.6 2.2 fusion.43
  84.9 35.8 %all_gather.13 = bf16[16,2048]{1,0:T(8,128)(2,1)S(1)} all-gather(bf16[16,128]{1,0:T(8,128)(2,1)S(1)} %convert_element_type.49), channel_id=1, replica_groups=mesh['cell'=16,'pre'=2] {'cell'}, dimensions={1}, use_global_device_ids=true | all-gather | bytes 69632 | tf_op jit(solution)/shard_map/all_gather | solution.py:32
  120.7 1.0 fusion.44
  121.7 0.2 reduce-scatter.9.cloned.1.call-start
  122.0 0.1 copy.37
  122.1 2.5 copy.77
  124.6 2.6 copy.39
  127.2 0.3 mul.199
  127.7 0.6 copy-done.4
  128.3 2.9 subtract_bitcast_fusion
  131.2 2.6 copy.52
  133.8 3.3 %fusion.7 = (bf16[16,128]{1,0:T(8,128)(2,1)S(1)}, f32[128,16,128]{2,0,1:T(8,128)}) fusion(f32[16,16,8,128]{3,2,1,0:T(8,128)} %get-tuple-element.32, f32[128,128]{1,0:T(8,128)S(1)} %fusion.29, f32[16,128,128]{2,1,0:T(8,128)S(1)} %bitcast.115, f32[128,128]{1,0:T(8,128)S(1)} %fusion.41), kind=kOutput, calls=%fused_computation.17 | convolution fusion | flops 403437568 | bytes 3280896 | tf_op jit(solution)/shard_map/dot_general | solution.py:26
  137.1 1.8 all_gather.14
  139.0 0.9 fusion.45
  140.0 1.9 multiply_subtract_fusion
  141.9 76.3 %reduce-scatter.9.cloned.1.call-done = f32[16,128]{1,0:T(8,128)} async-done(((f32[16,2048]{1,0:T(8,128)}), f32[16,128]{1,0:T(8,128)}) %reduce-scatter.9.cloned.1.call-update) | async-done | bytes 8208 | tf_op jit(solution)/shard_map/reduce_scatter | solution.py:46
  218.2 0.7 fusion.35
  218.9 1.3 copy.76
  220.2 2.5 copy.46
  222.7 2.6 multiply_reduce_fusion
  225.4 1.8 all_gather.15
  227.2 0.9 fusion.46
  228.2 2.2 fusion.13
  230.4 1.6 copy.48
  232.0 69.4 %reduce-scatter.11.cloned.1.call-done = f32[16,128]{1,0:T(8,128)} async-done(((f32[16,2048]{1,0:T(8,128)}), f32[16,128]{1,0:T(8,128)}) %reduce-scatter.11.cloned.1.call-update) | async-done | bytes 8208 | tf_op jit(solution)/shard_map/reduce_scatter | solution.py:46
  301.4 0.7 fusion.39
  302.2 1.6 copy.49
  (42 shorter events, 0.9 us)
Async XLA Ops:
  7.2 43.6 %copy-start = (bf16[256,2048]{1,0:T(8,128)(2,1)S(1)}, bf16[256,2048]{1,0:T(8,128)(2,1)}, u32[]{:S(2)}) copy-start(bf16[256,2048]{1,0:T(8,128)(2,1)} %param.17) | copy-start | bytes 3145732
  7.2 72.5 %reduce-scatter.5.cloned.1.call-start = ((), (), s32[]{:S(2)}) async-start(), calls=%async_computation.4 | async-start | bytes 24576 | tf_op jit(solution)/shard_map/reduce_scatter | solution.py:37
  50.8 28.9 %copy-start.1 = (f32[128,16,128]{2,1,0:T(8,128)S(1)}, f32[128,16,128]{2,1,0:T(8,128)}, u32[]{:S(2)}) copy-start(f32[128,16,128]{2,1,0:T(8,128)} %param.15) | copy-start | bytes 3145732
  51.8 0.7 copy-start.7
  51.8 75.4 %reduce-scatter.7.cloned.1.call-start = ((), (), s32[]{:S(2)}) async-start(), calls=%async_computation.5 | async-start | bytes 24576 | tf_op jit(solution)/shard_map/reduce_scatter | solution.py:37
  52.5 0.7 copy-start.8
  53.1 0.7 copy-start.9
  53.1 0.7 copy-start.12
  53.8 0.7 copy-start.10
  54.4 0.7 copy-start.11
  78.7 0.7 copy-start.5
  79.5 0.7 copy-start.6
  121.7 96.4 %reduce-scatter.9.cloned.1.call-start = ((), (), s32[]{:S(2)}) async-start(), calls=%async_computation.6 | async-start | bytes 139264 | tf_op jit(solution)/shard_map/reduce_scatter | solution.py:46
  127.6 0.7 copy-start.4
  131.2 2.6 copy-start.2
  139.9 161.5 %reduce-scatter.11.cloned.1.call-start = ((), (), s32[]{:S(2)}) async-start(), calls=%async_computation.7 | async-start | bytes 139264 | tf_op jit(solution)/shard_map/reduce_scatter | solution.py:46
  220.2 2.5 copy-start.3
Sparse Core Ops, SparseCore 0:
  51.9 3.4 reduce-scatter.4
  121.9 5.2 reduce-scatter.6
  140.0 78.0 reduce-scatter.8
  228.3 73.1 reduce-scatter.10
where the time goes:
time: 311 us; the launch traced here: 310 us
  waiting for transfers between devices  146 us (47%)
  blocking collectives  82.2 us (26%)
  other arithmetic  31.3 us (10%)
  local copies, waits for them, and re-layouts  21.4 us (7%)
  matrix products  15.3 us (5%)
  between operations  14 us (5%)
    reduce_scatter x2, waiting for transfers between devices, backward_drive(): lax.psum_scatter(partial_cols, 'cell', scatter_dimension=1, tiled=True)  146 us
    all_gather x2, blocking collectives, forward_drive(): lax.all_gather(activity, 'cell', axis=1, tiled=True)  78.5 us
    another operation x3, other arithmetic, tree_inverse(): lower = jnp.linalg.cholesky(system)  12.4 us
    unnamed x30, local copies, waits for them, and re-layouts  11.6 us
    another operation x2, other arithmetic, tree_inverse(): lax.linalg.triangular_solve(lower, ident, left_side=True, lower=True)  10.5 us
    dot_general x4, matrix products, apply_matrix(): jnp.dot(matrix, field.reshape(depth, trials * cells), precision=lax.Preci...  10.4 us
    dot_general x3, local copies, waits for them, and re-layouts, apply_matrix(): jnp.dot(matrix, field.reshape(depth, trials * cells), precision=lax.Preci...  7.73 us
  transfers between devices with their start and end apart: 4, of which 2 were waited for; matrix products, arithmetic and copies ran while one was open for 11% of the time, Pallas kernels for 0%

commit v1 on v0

v1 whole, which is shorter than its diff:
```python
import functools

import jax
import jax.numpy as jnp
from jax import lax
from jax.experimental import pallas as pl
from jax.experimental.pallas import tpu as pltpu
from jax.sharding import PartitionSpec as P

f32 = jnp.float32
bf16 = jnp.bfloat16
reversal = 1.0
reach = 8
sweeps = 20
return_dtype = jnp.float32


def split_rows(x):
    hi = x.astype(bf16)
    lo = (x - hi.astype(f32)).astype(bf16)
    return jnp.concatenate([hi, hi, lo], axis=0)


def split_cols(x):
    hi = x.astype(bf16)
    lo = (x - hi.astype(f32)).astype(bf16)
    return jnp.concatenate([hi, lo, hi], axis=1)


def dot3(left, right):
    return jnp.dot(left, right, preferred_element_type=f32)


def tree_inverse(parent, axial, cap):
    n = parent.shape[1]
    lane = lax.broadcasted_iota(jnp.int32, (1, n), 1)
    shifts = [(n - j) % n for j in range(1, min(reach, n - 1) + 1)]

    def rolled(x, s):
        return pltpu.roll(jnp.broadcast_to(x, (8, n)), s, axis=1)[0:1]

    children = []
    for j, s in enumerate(shifts, 1):
        is_child = (rolled(parent, s) == lane) & (lane + j < n)
        children.append(jnp.where(is_child, 1.0, 0.0))
    root = lane == 0
    base = cap + jnp.where(root, axial, 0.0)

    def sweep(_, x):
        g = axial * x / (x + axial)
        g = jnp.where(root, 0.0, g)
        parts = [m * rolled(g, s) for m, s in zip(children, shifts)]
        while len(parts) > 1:
            parts = [sum(parts[k : k + 2]) for k in range(0, len(parts), 2)]
        return base + parts[0]

    x = lax.fori_loop(0, sweeps, sweep, base)
    d = x + jnp.where(root, 0.0, axial)
    f = jnp.where(root, 0.0, axial / d)
    up = lax.broadcasted_iota(jnp.int32, (n, n), 0)
    across = lax.broadcasted_iota(jnp.int32, (n, n), 1)
    power = jnp.where(jnp.broadcast_to(parent, (n, n)) == up, jnp.broadcast_to(f, (n, n)), 0.0)
    total = jnp.where(up == across, 1.0, 0.0) + power
    power = dot3(split_cols(power), split_rows(power))
    width = 2
    while width < n:
        left = split_cols(power)
        if 2 * width < n:
            both = dot3(left, split_rows(jnp.concatenate([total, power], axis=1)))
            total, power = total + both[:, :n], both[:, n:]
        else:
            total = total + dot3(left, split_rows(total))
        width *= 2
    dinv = jnp.broadcast_to(1.0 / d, (n, n)).T
    return dot3(split_cols(total.T), split_rows(dinv * total))


def kernel(
    C, R,
    v_hbm, cot_hbm, w_hbm, leak_ref, drive_ref, site_ref, parent_ref, axial_ref, cap_ref, bank_ref, sched_ref,
    vout_hbm, gout_hbm,
    v_vm, cot_vm, w_vm, vo_vm, go_vm, B, P1, E,
    pat, rows, act, part_f, got_f, sa, part_b, got_b,
    cell_send, cell_recv, pre_send, pre_recv, local,
):
    a = lax.axis_index("cell")
    b = lax.axis_index("pre")
    n = parent_ref.shape[1]
    T = sched_ref.shape[1]
    L = leak_ref.shape[1]
    MESH = pl.DeviceIdType.MESH
    cells = [lax.rem(a + j, C) for j in range(C)]
    pres = [lax.rem(b + j, R) for j in range(R)]

    first = pltpu.make_async_copy(v_hbm.at[pl.ds(0, T)], v_vm.at[pl.ds(0, T)], local.at[0])
    rest = pltpu.make_async_copy(v_hbm.at[pl.ds(T, (n - 1) * T)], v_vm.at[pl.ds(T, (n - 1) * T)], local.at[1])
    cot_in = pltpu.make_async_copy(cot_hbm, cot_vm, local.at[2])
    w_in = pltpu.make_async_copy(w_hbm, w_vm, local.at[3])
    for c in (first, rest, w_in, cot_in):
        c.start()

    barrier = pltpu.get_barrier_semaphore()
    for j in range(1, C):
        pl.semaphore_signal(barrier, inc=1, device_id=(cells[j], b), device_id_type=MESH)
    for j in range(1, R):
        pl.semaphore_signal(barrier, inc=1, device_id=(a, pres[j]), device_id_type=MESH)
    pl.semaphore_wait(barrier, C - 1 + R - 1)

    def to_cells(phase, source, target):
        copies = []
        for j in range(1, C):
            copies.append(pltpu.make_async_remote_copy(
                src_ref=source(cells[j]), dst_ref=target(j),
                send_sem=cell_send.at[phase, j], recv_sem=cell_recv.at[phase, j],
                device_id=(cells[j], b), device_id_type=MESH))
        for c in copies:
            c.start()
        return copies

    def to_pres(phase, source, target):
        copies = []
        for j in range(1, R):
            copies.append(pltpu.make_async_remote_copy(
                src_ref=source(pres[j]), dst_ref=target(j),
                send_sem=pre_send.at[phase, j], recv_sem=pre_recv.at[phase, j],
                device_id=(a, pres[j]), device_id_type=MESH))
        for c in copies:
            c.start()
        return copies

    sent = []

    def arrived(copies):
        for c in copies:
            c.wait_recv()
        sent.extend(copies)

    def share_activity(moment, rates):
        act[moment, a] = rates.astype(bf16)
        return to_cells(moment, lambda _: act.at[moment, a], lambda j: act.at[moment, a])

    def forward(moment, copies):
        arrived(copies)
        gathered = jnp.concatenate([act[moment, j] for j in range(C)], axis=1)
        partial = lax.dot_general(gathered, w_vm[...], (((1,), (1,)), ((), ())), preferred_element_type=f32)
        for r in range(R):
            part_f[moment, r] = partial[:, r * L : (r + 1) * L]
        return to_pres(moment, lambda r: part_f.at[moment, r], lambda j: got_f.at[moment, j])

    def forward_sum(moment, copies):
        arrived(copies)
        total = part_f[moment, b]
        for j in range(1, R):
            total = total + got_f[moment, j]
        return total

    def share_site(moment, value):
        sa[moment, b] = value.astype(bf16)
        return to_pres(2 + moment, lambda _: sa.at[moment, b], lambda j: sa.at[moment, b])

    def backward(moment, copies):
        arrived(copies)
        gathered = jnp.concatenate([sa[moment, r] for r in range(R)], axis=1)
        partial = jnp.dot(gathered, w_vm[...], preferred_element_type=f32)
        for j in range(C):
            part_b[moment, j] = partial[:, j * L : (j + 1) * L].astype(part_b.dtype)
        return to_cells(2 + moment, lambda q: part_b.at[moment, q], lambda j: got_b.at[moment, j])

    def backward_sum(moment, copies):
        arrived(copies)
        parts = [part_b[moment, a].astype(f32)] + [got_b[moment, j].astype(f32) for j in range(1, C)]
        while len(parts) > 1:
            parts = [sum(parts[k : k + 2]) for k in range(0, len(parts), 2)]
        return parts[0]

    def sigmoid(x):
        return 1.0 / (1.0 + jnp.exp(-x))

    first.wait()
    r0 = sigmoid(v_vm[0:T])
    ag0 = share_activity(0, r0)

    inverse = tree_inverse(parent_ref[...], axial_ref[...], cap_ref[...])
    left = split_cols(inverse)
    cap_col = jnp.broadcast_to(cap_ref[...], (n, n)).T
    levels = cap_col[:, :L] - leak_ref[...]
    drive = drive_ref[...]
    mask = jnp.where(site_ref[...] == lax.broadcasted_iota(jnp.int32, (n, L), 0), 1.0, 0.0)
    inv_site = dot3(left, split_rows(mask))
    inv_root = inv_site[0:1]
    inv_own = jnp.sum(mask * inv_site, axis=0, keepdims=True)
    pat[...] = jnp.zeros_like(pat)
    for moment in range(2):
        for t in range(T):
            pat[pl.ds(moment * T + t, 1)] = bank_ref[pl.ds(sched_ref[moment, t], 1)]
    pattern = pat[...].T

    def strided(t):
        return pl.ds(t, n, stride=T)

    def apply(blocks):
        out = dot3(left, split_rows(jnp.concatenate(blocks, axis=1)))
        return [out[:, k * L : (k + 1) * L] for k in range(len(blocks))]

    V0s, Bs, B0, P1s, Es, U0, U1, Q1, W1, S0 = range(10)

    def at_site(x):
        return jnp.sum(mask * x, axis=0, keepdims=True)

    group = 2 if T % 2 == 0 else 1
    rest.wait()
    for t0 in range(0, T, group):
        totals = []
        for t in range(t0, t0 + group):
            x = v_vm[strided(t)]
            rows[V0s, pl.ds(t, 1)] = at_site(x)
            totals.append(levels * x + pattern[:, t : t + 1] * drive)
        for t, y in zip(range(t0, t0 + group), apply(totals)):
            B[t] = y
            rows[Bs, pl.ds(t, 1)] = at_site(y)
            rows[B0, pl.ds(t, 1)] = y[0:1]
    cot_in.wait()
    for t0 in range(0, T, group):
        for t, y in zip(range(t0, t0 + group), apply([cot_vm[strided(t)] for t in range(t0, t0 + group)])):
            P1[t] = y
            rows[P1s, pl.ds(t, 1)] = at_site(y)

    w_in.wait()
    syn0 = forward_sum(0, forward(0, ag0))
    u0 = syn0 * (reversal - rows[V0s])
    v1_root = rows[B0] + inv_root * u0
    v1_own = rows[Bs] + inv_own * u0
    r1 = sigmoid(v1_root)
    ag1 = share_activity(1, r1)
    rs1 = backward(1, share_site(1, rows[P1s] * (reversal - v1_own)))
    rows[U0] = u0
    rows[S0] = syn0

    for t0 in range(0, T, group):
        for t, y in zip(range(t0, t0 + group), apply([levels * P1[t] for t in range(t0, t0 + group)])):
            E[t] = y
            rows[Es, pl.ds(t, 1)] = at_site(y)

    syn1 = forward_sum(1, forward(1, ag1))
    rows[U1] = syn1 * (reversal - v1_own)
    q1 = syn1 * rows[P1s]
    ret1 = backward_sum(1, rs1)
    w1 = ret1 * r1 * (1.0 - r1)
    rs0 = backward(0, share_site(0, (rows[Es] - inv_own * q1 + inv_root * w1) * (reversal - rows[V0s])))
    rows[Q1] = q1
    rows[W1] = w1

    inv_col = jnp.broadcast_to(inverse[:, 0:1], (n, L))
    for t in range(T):
        pulled = E[t] - inv_site * rows[Q1, pl.ds(t, 1)] + inv_col * rows[W1, pl.ds(t, 1)]
        go_vm[strided(t)] = levels * pulled - mask * rows[S0, pl.ds(t, 1)] * pulled
    g_out = pltpu.make_async_copy(go_vm.at[pl.ds(T, (n - 1) * T)], gout_hbm.at[pl.ds(T, (n - 1) * T)], local.at[4])
    g_out.start()
    for t0 in range(0, T, group):
        totals = []
        for t in range(t0, t0 + group):
            v1 = B[t] + inv_site * rows[U0, pl.ds(t, 1)]
            totals.append(levels * v1 + pattern[:, T + t : T + t + 1] * drive)
        for t, y in zip(range(t0, t0 + group), apply(totals)):
            vo_vm[strided(t)] = y + inv_site * rows[U1, pl.ds(t, 1)]
    v_out = pltpu.make_async_copy(vo_vm, vout_hbm, local.at[5])
    v_out.start()

    ret0 = backward_sum(0, rs0)
    go_vm[0:T] = go_vm[0:T] + ret0 * r0 * (1.0 - r0)
    g_last = pltpu.make_async_copy(go_vm.at[pl.ds(0, T)], gout_hbm.at[pl.ds(0, T)], local.at[6])
    g_last.start()
    for c in sent:
        c.wait_send()
    for c in (g_out, v_out, g_last):
        c.wait()


def body(C, R, v_init, cotangent, weights, leak, drive, site, parent, axial, cap, bank, sched):
    n, T, L = v_init.shape
    flat = (n * T, L)
    anywhere = pl.BlockSpec(memory_space=pl.ANY)
    near = pl.BlockSpec(memory_space=pltpu.VMEM)
    slab = pltpu.VMEM((T, n, L), f32)
    v_final, v_grad = pl.pallas_call(
        functools.partial(kernel, C, R),
        out_shape=(jax.ShapeDtypeStruct(flat, f32),) * 2,
        in_specs=[anywhere] * 3 + [near] * 7 + [pl.BlockSpec(memory_space=pltpu.SMEM)],
        out_specs=(anywhere, anywhere),
        scratch_shapes=[
            pltpu.VMEM(flat, f32), pltpu.VMEM(flat, f32), pltpu.VMEM(weights.shape, bf16),
            pltpu.VMEM(flat, f32), pltpu.VMEM(flat, f32), slab, slab, slab,
            pltpu.VMEM((n, n), f32), pltpu.VMEM((10, T, L), f32),
            pltpu.VMEM((2, C, T, L), bf16),
            pltpu.VMEM((2, R, T, L), f32), pltpu.VMEM((2, R, T, L), f32),
            pltpu.VMEM((2, R, T, L), bf16),
            pltpu.VMEM((2, C, T, L), return_dtype), pltpu.VMEM((2, C, T, L), return_dtype),
            pltpu.SemaphoreType.DMA((4, C)), pltpu.SemaphoreType.DMA((4, C)),
            pltpu.SemaphoreType.DMA((4, R)), pltpu.SemaphoreType.DMA((4, R)),
            pltpu.SemaphoreType.DMA((7,)),
        ],
        compiler_params=pltpu.CompilerParams(collective_id=0, has_side_effects=True),
    )(
        v_init.reshape(flat), cotangent.reshape(flat), weights,
        leak.reshape(1, L), drive.reshape(1, L), site.reshape(1, L),
        parent.reshape(1, n), axial.reshape(1, n), cap.reshape(1, n), bank, sched,
    )
    return v_final.reshape(n, T, L), v_grad.reshape(n, T, L)


def solution(mesh):
    own = P(("cell", "pre"))
    field = P(None, None, ("cell", "pre"))
    in_specs = (field, field, P("cell", "pre"), own, own, own, P(), P(), P(), P(), P())
    sizes = mesh.shape["cell"], mesh.shape["pre"]
    return jax.shard_map(
        functools.partial(body, *sizes), mesh=mesh, in_specs=in_specs, out_specs=(field, field), check_vma=False
    )
```

time: 311 us -> 32.9 us (0.11)
  waiting for transfers between devices: 146 us -> 0 us
  blocking collectives: 82.2 us -> 0 us
  other arithmetic: 31.3 us -> 0 us
  Pallas kernels: 0 us -> 28.7 us
  local copies, waits for them, and re-layouts: 21.4 us -> 3.32 us
  matrix products: 15.3 us -> 0 us
  between operations: 14 us -> 0.65 us
    reduce_scatter x4 -> x0, waiting for transfers between devices: 146 us -> none  [the longest x2 146 us: backward_drive(): lax.psum_scatter(partial_cols, 'cell', scatter_dimension=1, tiled=True)]
    all_gather x4 -> x0, blocking collectives: 82.2 us -> none  [the longest x2 78.5 us: forward_drive(): lax.all_gather(activity, 'cell', axis=1, tiled=True)]
    pallas_call x0 -> x1, Pallas kernels: none -> 28.7 us  [body(): pl.pallas_call(functools.partial(kernel, C, R), out_shape=(jax.ShapeDtype...]
    another operation x5 -> x0, other arithmetic: 22.9 us -> none  [the longest x3 12.4 us: tree_inverse(): lower = jnp.linalg.cholesky(system)]
    dot_general x12 -> x0, matrix products: 15.1 us -> none  [the longest x4 10.4 us: apply_matrix(): jnp.dot(matrix, field.reshape(depth, trials * cells), precision=lax.Preci...]
    unnamed x30 -> x4, local copies, waits for them, and re-layouts: 11.6 us -> 3.32 us
    dot_general x4 -> x0, local copies, waits for them, and re-layouts: 7.82 us -> none  [the longest x3 7.73 us: apply_matrix(): jnp.dot(matrix, field.reshape(depth, trials * cells), precision=lax.Preci...]
  transfers between devices with their start and end apart: 4 -> 0, of which waited for: 2 -> 0; matrix products, arithmetic and copies ran while one was open for 11% -> 0% of each run, Pallas kernels for 0% -> 0%
where the time goes in v1:
time: 32.9 us; the launch traced here: 32.7 us
  Pallas kernels  28.7 us (87%)
  local copies, waits for them, and re-layouts  3.32 us (10%)
  between operations  0.65 us (2%)
    pallas_call x1, Pallas kernels, body(): pl.pallas_call(functools.partial(kernel, C, R), out_shape=(jax.ShapeDtype...  28.7 us
    unnamed x4, local copies, waits for them, and re-layouts  3.32 us

profile of v1, /device:TPU:0, one launch (start us, length us, event | category | flops | bytes accessed | tf_op | source)
XLA Modules:
  0.0 32.7 jit_solution(523289101148767816)
XLA Ops:
  0.6 28.7 %shard_map.122 = (f32[2048,128]{1,0:T(8,128)}, f32[2048,128]{1,0:T(8,128)}) custom-call(f32[2048,128]{1,0:T(8,128)} %bitcast.10, f32[2048,128]{1,0:T(8,128)} %bitcast.11, bf16[256,2048]{1,0:T(8,128)(2,1)} %w_hbm.1, f32[1,128]{1,0:T(1,128)} %bitcast.14, f32[1,128]{1,0:T(1,128)} %bitcast.15, s32[1,128]{1,0:T(1,128)} %bitcast.16, s32[1,128]{1,0:T(1,128)} %bitcast.17, ...), custom_call_target="tpu_custom_call" | custom-call | tf_op jit(solution)/shard_map/pallas_call | solution.py:285
  29.4 0.0 copy-start
  29.4 2.4 %copy.15 = f32[128,16,128]{2,1,0:T(8,128)} copy(f32[128,16,128]{2,1,0:T(8,128)} %bitcast.13) | data formatting | bytes 2097152
  31.7 0.0 copy-done
  31.7 1.0 %copy.16 = f32[128,16,128]{2,1,0:T(8,128)} copy(f32[128,16,128]{2,1,0:T(8,128)S(1)} %bitcast.12) | data formatting | bytes 2097152
Async XLA Ops:
  29.4 2.4 %copy-start = (f32[2048,128]{1,0:T(8,128)S(1)}, f32[2048,128]{1,0:T(8,128)}, u32[]{:S(2)}) copy-start(f32[2048,128]{1,0:T(8,128)} %get-tuple-element.5) | copy-start | bytes 3145732

commit v2 on v1

--- a/solution.py
+++ b/solution.py
@@ -12,7 +12,7 @@
 reversal = 1.0
 reach = 8
 sweeps = 20
-return_dtype = jnp.float32
+return_dtype = jnp.bfloat16
 
 
 def split_rows(x):
@@ -78,8 +78,8 @@
 def kernel(
     C, R,
     v_hbm, cot_hbm, w_hbm, leak_ref, drive_ref, site_ref, parent_ref, axial_ref, cap_ref, bank_ref, sched_ref,
-    vout_hbm, gout_hbm,
-    v_vm, cot_vm, w_vm, vo_vm, go_vm, B, P1, E,
+    vo_vm, go_vm,
+    v_vm, cot_vm, w_vm, B, P1, E,
     pat, rows, act, part_f, got_f, sa, part_b, got_b,
     cell_send, cell_recv, pre_send, pre_recv, local,
 ):
@@ -91,6 +91,7 @@
     MESH = pl.DeviceIdType.MESH
     cells = [lax.rem(a + j, C) for j in range(C)]
     pres = [lax.rem(b + j, R) for j in range(R)]
+    near_first = sorted(range(1, C), key=lambda j: min(j, C - j))
 
     first = pltpu.make_async_copy(v_hbm.at[pl.ds(0, T)], v_vm.at[pl.ds(0, T)], local.at[0])
     rest = pltpu.make_async_copy(v_hbm.at[pl.ds(T, (n - 1) * T)], v_vm.at[pl.ds(T, (n - 1) * T)], local.at[1])
@@ -104,11 +105,10 @@
         pl.semaphore_signal(barrier, inc=1, device_id=(cells[j], b), device_id_type=MESH)
     for j in range(1, R):
         pl.semaphore_signal(barrier, inc=1, device_id=(a, pres[j]), device_id_type=MESH)
-    pl.semaphore_wait(barrier, C - 1 + R - 1)
 
     def to_cells(phase, source, target):
         copies = []
-        for j in range(1, C):
+        for j in near_first:
             copies.append(pltpu.make_async_remote_copy(
                 src_ref=source(cells[j]), dst_ref=target(j),
                 send_sem=cell_send.at[phase, j], recv_sem=cell_recv.at[phase, j],
@@ -178,6 +178,7 @@
 
     first.wait()
     r0 = sigmoid(v_vm[0:T])
+    pl.semaphore_wait(barrier, C - 1 + R - 1)
     ag0 = share_activity(0, r0)
 
     inverse = tree_inverse(parent_ref[...], axial_ref[...], cap_ref[...])
@@ -231,17 +232,19 @@
     v1_root = rows[B0] + inv_root * u0
     v1_own = rows[Bs] + inv_own * u0
     r1 = sigmoid(v1_root)
+    site1 = share_site(1, rows[P1s] * (reversal - v1_own))
     ag1 = share_activity(1, r1)
-    rs1 = backward(1, share_site(1, rows[P1s] * (reversal - v1_own)))
+    rs1 = backward(1, site1)
     rows[U0] = u0
     rows[S0] = syn0
 
+    swap1 = forward(1, ag1)
     for t0 in range(0, T, group):
         for t, y in zip(range(t0, t0 + group), apply([levels * P1[t] for t in range(t0, t0 + group)])):
             E[t] = y
             rows[Es, pl.ds(t, 1)] = at_site(y)
 
-    syn1 = forward_sum(1, forward(1, ag1))
+    syn1 = forward_sum(1, swap1)
     rows[U1] = syn1 * (reversal - v1_own)
     q1 = syn1 * rows[P1s]
     ret1 = backward_sum(1, rs1)
@@ -254,8 +257,6 @@
     for t in range(T):
         pulled = E[t] - inv_site * rows[Q1, pl.ds(t, 1)] + inv_col * rows[W1, pl.ds(t, 1)]
         go_vm[strided(t)] = levels * pulled - mask * rows[S0, pl.ds(t, 1)] * pulled
-    g_out = pltpu.make_async_copy(go_vm.at[pl.ds(T, (n - 1) * T)], gout_hbm.at[pl.ds(T, (n - 1) * T)], local.at[4])
-    g_out.start()
     for t0 in range(0, T, group):
         totals = []
         for t in range(t0, t0 + group):
@@ -263,16 +264,18 @@
             totals.append(levels * v1 + pattern[:, T + t : T + t + 1] * drive)
         for t, y in zip(range(t0, t0 + group), apply(totals)):
             vo_vm[strided(t)] = y + inv_site * rows[U1, pl.ds(t, 1)]
-    v_out = pltpu.make_async_copy(vo_vm, vout_hbm, local.at[5])
-    v_out.start()
 
     ret0 = backward_sum(0, rs0)
     go_vm[0:T] = go_vm[0:T] + ret0 * r0 * (1.0 - r0)
-    g_last = pltpu.make_async_copy(go_vm.at[pl.ds(0, T)], gout_hbm.at[pl.ds(0, T)], local.at[6])
-    g_last.start()
     for c in sent:
         c.wait_send()
-    for c in (g_out, v_out, g_last):
+
+
+def write_out(v_ref, g_ref, v_hbm, g_hbm, sems):
+    copies = [pltpu.make_async_copy(v_ref, v_hbm, sems.at[0]), pltpu.make_async_copy(g_ref, g_hbm, sems.at[1])]
+    for c in copies:
+        c.start()
+    for c in copies:
         c.wait()
 
 
@@ -282,14 +285,14 @@
     anywhere = pl.BlockSpec(memory_space=pl.ANY)
     near = pl.BlockSpec(memory_space=pltpu.VMEM)
     slab = pltpu.VMEM((T, n, L), f32)
-    v_final, v_grad = pl.pallas_call(
+    held = pl.pallas_call(
         functools.partial(kernel, C, R),
-        out_shape=(jax.ShapeDtypeStruct(flat, f32),) * 2,
+        out_shape=(pltpu.VMEM(flat, f32),) * 2,
         in_specs=[anywhere] * 3 + [near] * 7 + [pl.BlockSpec(memory_space=pltpu.SMEM)],
-        out_specs=(anywhere, anywhere),
+        out_specs=(near, near),
         scratch_shapes=[
             pltpu.VMEM(flat, f32), pltpu.VMEM(flat, f32), pltpu.VMEM(weights.shape, bf16),
-            pltpu.VMEM(flat, f32), pltpu.VMEM(flat, f32), slab, slab, slab,
+            slab, slab, slab,
             pltpu.VMEM((n, n), f32), pltpu.VMEM((10, T, L), f32),
             pltpu.VMEM((2, C, T, L), bf16),
             pltpu.VMEM((2, R, T, L), f32), pltpu.VMEM((2, R, T, L), f32),
@@ -297,7 +300,7 @@
             pltpu.VMEM((2, C, T, L), return_dtype), pltpu.VMEM((2, C, T, L), return_dtype),
             pltpu.SemaphoreType.DMA((4, C)), pltpu.SemaphoreType.DMA((4, C)),
             pltpu.SemaphoreType.DMA((4, R)), pltpu.SemaphoreType.DMA((4, R)),
-            pltpu.SemaphoreType.DMA((7,)),
+            pltpu.SemaphoreType.DMA((4,)),
         ],
         compiler_params=pltpu.CompilerParams(collective_id=0, has_side_effects=True),
     )(
@@ -305,6 +308,13 @@
         leak.reshape(1, L), drive.reshape(1, L), site.reshape(1, L),
         parent.reshape(1, n), axial.reshape(1, n), cap.reshape(1, n), bank, sched,
     )
+    v_final, v_grad = pl.pallas_call(
+        write_out,
+        out_shape=(jax.ShapeDtypeStruct(flat, f32),) * 2,
+        in_specs=[near] * 2,
+        out_specs=(anywhere, anywhere),
+        scratch_shapes=[pltpu.SemaphoreType.DMA((2,))],
+    )(*[pltpu.with_memory_space_constraint(x, pltpu.VMEM) for x in held])
     return v_final.reshape(n, T, L), v_grad.reshape(n, T, L)
 
 

time: 32.9 us -> 29.3 us (0.89)
  local copies, waits for them, and re-layouts: 3.32 us -> 0 us
    unnamed x4 -> x0, local copies, waits for them, and re-layouts: 3.32 us -> none
    pallas_call x1 -> x2, Pallas kernels: 28.7 us -> 28.4 us  [the longest x1 27.1 us: body(): pl.pallas_call(functools.partial(kernel, C, R), out_shape=(pltpu.VMEM(fla...]
where the time goes in v2:
time: 29.3 us; the launch traced here: 29.1 us
  Pallas kernels  28.4 us (97%)
  between operations  0.64 us (2%)
    pallas_call x1, Pallas kernels, body(): pl.pallas_call(functools.partial(kernel, C, R), out_shape=(pltpu.VMEM(fla...  27.1 us
    pallas_call x1, Pallas kernels, body(): pl.pallas_call(write_out, out_shape=(jax.ShapeDtypeStruct(flat, f32),) *...  1.33 us

profile of v2, /device:TPU:0, one launch (start us, length us, event | category | flops | bytes accessed | tf_op | source)
XLA Modules:
  0.0 29.1 jit_solution(15940526251227396965)
XLA Ops:
  0.6 27.1 %shard_map.122 = (f32[2048,128]{1,0:T(8,128)S(1)}, f32[2048,128]{1,0:T(8,128)S(1)}) custom-call(f32[2048,128]{1,0:T(8,128)} %bitcast.10, f32[2048,128]{1,0:T(8,128)} %bitcast.11, bf16[256,2048]{1,0:T(8,128)(2,1)} %w_hbm.1, f32[1,128]{1,0:T(1,128)} %bitcast.12, f32[1,128]{1,0:T(1,128)} %bitcast.13, s32[1,128]{1,0:T(1,128)} %bitcast.14, s32[1,128]{1,0:T(1,128)} %bitcast.15, ...), custom_call_target="tpu_custom_call" | custom-call | tf_op jit(solution)/shard_map/pallas_call | solution.py:288
  27.7 1.3 %shard_map.123 = (f32[2048,128]{1,0:T(8,128)}, f32[2048,128]{1,0:T(8,128)}) custom-call(f32[2048,128]{1,0:T(8,128)S(1)} %get-tuple-element.6.v_ref, f32[2048,128]{1,0:T(8,128)S(1)} %get-tuple-element.7.g_ref), custom_call_target="tpu_custom_call" | custom-call | tf_op jit(solution)/shard_map/pallas_call | solution.py:311
